TPU v7x, 512 devices: a whole 4x8x8 slice. The times are simulated.
512 devices in a mesh: dp: 16 (over x, y_lo, core), pipe: 8 (over z), tensor: 4 (over y_hi).
Axes of the slice: x: 4, y: 8 (y_hi: 4, y_lo: 2; y = y_hi * 2 + y_lo), z: 8, core: 2. Of those that a mesh axis runs over, the one named last changes fastest.
Arguments:
- weights: bfloat16 [11264, 1408], P(('dp', 'pipe', 'tensor')), may hold values from -6 to 6
- first_moment: bfloat16 [11264, 1408], P(('dp', 'pipe', 'tensor')), may hold values from -6 to 6
- second_moment: bfloat16 [11264, 1408], P(('dp', 'pipe', 'tensor')), may hold values from 0.049804688 to 5
- row_weight: float32 [1408], replicated, may hold values from -1 to 1
- col_weight: float32 [1408], replicated, may hold values from 1 to 4
Outputs:
- weight_tiles: bfloat16 [11264, 1408], P(('pipe', 'tensor'))
- first_tiles: bfloat16 [11264, 1408], P(('pipe', 'tensor'))
- second_tiles: bfloat16 [11264, 1408], P(('pipe', 'tensor'))
- checksums: float32 [3, 8, 4, 11], P(None, 'pipe', 'tensor')
All inputs are finite; a program needn't handle non-finite values.
Results may differ from a plain program's by a relative error of at most 0.001.
Values may be sent and summed in bfloat16 or wider, within the bound.
A program may use at most 64 MiB of HBM per device.

v0:
```python
import jax
import jax.numpy as jnp
from jax import lax
from jax.sharding import Mesh
from jax.sharding import PartitionSpec as P

CHECK_COLS = 128
DP = ("dp_0", "dp_1", "dp_2")
DP_PIPE_TENSOR = ("dp_0", "dp_1", "dp_2", "pipe", "tensor")


def for_sending(array):
    return jax.tree.map(lambda a: a.astype(jnp.bfloat16) if a.dtype == jnp.float32 else a, array)


def laid_out(blocks, dim):
    dims = list(blocks.shape[1:])
    dims[dim] *= blocks.shape[0]
    return jnp.moveaxis(blocks, 0, dim).reshape(dims)


def gather_in_order(array, axes, order):
    blocks = array[None]
    for k in order:
        blocks = lax.all_gather(blocks, axes[k], axis=0, tiled=True)
    block = [lax.axis_size(axes[k]) for k in reversed(order)]
    blocks = blocks.reshape(*block, *array.shape)
    turned = sorted(range(len(order)), key=lambda place: order[len(order) - 1 - place])
    return blocks.transpose(*turned, *range(len(order), blocks.ndim)).reshape(-1, *array.shape)


def gather_axes(array, axes, order, dim):
    return laid_out(gather_in_order(array, axes, order), dim)


def column_sums(data, row_part, col_weight, col_blocks):
    row_mixed = jnp.dot(
        row_part[None, :], data.astype(jnp.float32), precision=lax.Precision.HIGHEST
    )[0]
    return jnp.sum((row_mixed * col_weight).reshape(col_blocks, -1), axis=1)


def shards(weights, first_moment, second_moment, row_weight, col_weight):
    dp_count = lax.axis_size(DP)
    pipe_count = lax.axis_size("pipe")
    tensor_count = lax.axis_size("tensor")
    shard_rows, width = weights.shape
    dp_section = dp_count // pipe_count
    tile_shards = dp_count // tensor_count
    piece_cols = width // dp_count
    tile_rows = shard_rows * dp_count
    col_blocks = width // CHECK_COLS
    factor = float(tile_rows * CHECK_COLS) ** (-0.5)
    sources = (weights, first_moment, second_moment)
    exchanged = (
        lax.all_to_all(sources[0], DP, split_axis=1, concat_axis=0, tiled=True),
        lax.all_to_all(sources[1], DP, split_axis=1, concat_axis=0, tiled=True),
        lax.all_to_all(sources[2], DP, split_axis=1, concat_axis=0, tiled=True),
    )
    grouped = tuple(
        (item.reshape(pipe_count, dp_section, shard_rows, piece_cols) for item in exchanged)
    )
    sectioned = jax.tree.map(
        lambda part, own: part.astype(own.dtype),
        lax.all_to_all(for_sending(grouped), "pipe", split_axis=0, concat_axis=2, tiled=True),
        grouped,
    )
    routed = tuple(
        (item.reshape(tensor_count, tile_shards, 1, shard_rows, piece_cols) for item in sectioned)
    )
    arrived = jax.tree.map(
        lambda part, own: part.astype(own.dtype),
        lax.all_to_all(for_sending(routed), "tensor", split_axis=0, concat_axis=2, tiled=True),
        routed,
    )
    flat_pieces = tuple((item.reshape(tile_rows, piece_cols) for item in arrived))
    tiles = jax.tree.map(
        lambda part, own: part.astype(own.dtype),
        jax.tree.map(lambda part: gather_axes(part, DP, (1, 0, 2), 1), for_sending(flat_pieces)),
        flat_pieces,
    )
    tensor_pos = lax.axis_index("tensor")
    row_part = lax.dynamic_slice_in_dim(row_weight, tensor_pos * tile_rows, tile_rows)
    local_sums = jnp.stack([column_sums(item, row_part, col_weight, col_blocks) for item in tiles])
    checks = (local_sums * factor).reshape(3, 1, 1, col_blocks)
    return (tiles[0], tiles[1], tiles[2], checks)


def solution(mesh):
    finer = Mesh(
        mesh.devices.reshape(4, 2, 2, mesh.shape["pipe"], mesh.shape["tensor"]),
        ("dp_0", "dp_1", "dp_2", "pipe", "tensor"),
    )
    in_specs = (P(DP_PIPE_TENSOR, None), P(DP_PIPE_TENSOR, None), P(DP_PIPE_TENSOR, None), P(), P())
    out_specs = (
        P(("pipe", "tensor"), None),
        P(("pipe", "tensor"), None),
        P(("pipe", "tensor"), None),
        P(None, "pipe", "tensor", None),
    )
    return jax.shard_map(
        shards, mesh=finer, in_specs=in_specs, out_specs=out_specs, check_vma=False
    )
```

profile of v0, /device:TPU:1, one launch (start us, length us, event | category | flops | bytes accessed | tf_op | source)
XLA Modules:
  0.0 177.1 jit_solution(7908738768736243178)
XLA Ops:
  0.6 0.0 copy-start
  0.6 1.1 all_to_all.102
  1.7 0.7 copy.84
  2.4 10.1 %all-to-all-start = ((bf16[22,16,88]{2,0,1:T(8,128)(2,1)}), bf16[22,16,88]{2,0,1:T(8,128)(2,1)S(1)}, u32[]{:S(2)}, u32[]{:S(2)}) async-start(bf16[22,16,88]{2,0,1:T(8,128)(2,1)} %copy.84), calls=%async_computation | async-start | bytes 196608 | tf_op jit(solution)/shard_map/all_to_all | solution.py:56
  12.5 1.1 all_to_all.111
  13.6 0.7 copy.92
  14.3 4.2 %all-to-all-done = bf16[22,16,88]{2,0,1:T(8,128)(2,1)S(1)} async-done(((bf16[22,16,88]{2,0,1:T(8,128)(2,1)}), bf16[22,16,88]{2,0,1:T(8,128)(2,1)S(1)}, u32[]{:S(2)}, u32[]{:S(2)}) %all-to-all-start) | async-done | bytes 61984 | tf_op jit(solution)/shard_map/all_to_all | solution.py:56
  18.4 3.9 %all-to-all-start.3 = ((bf16[22,16,88]{2,0,1:T(8,128)(2,1)}), bf16[22,16,88]{2,0,1:T(8,128)(2,1)S(1)}, u32[]{:S(2)}, u32[]{:S(2)}) async-start(bf16[22,16,88]{2,0,1:T(8,128)(2,1)} %copy.92), calls=%async_computation.3 | async-start | bytes 196608 | tf_op jit(solution)/shard_map/all_to_all | solution.py:57
  22.3 0.0 copy-done
  22.3 0.2 all_to_all.120
  22.5 0.7 copy.100
  23.2 5.0 %all-to-all-done.3 = bf16[22,16,88]{2,0,1:T(8,128)(2,1)S(1)} async-done(((bf16[22,16,88]{2,0,1:T(8,128)(2,1)}), bf16[22,16,88]{2,0,1:T(8,128)(2,1)S(1)}, u32[]{:S(2)}, u32[]{:S(2)}) %all-to-all-start.3) | async-done | bytes 61984 | tf_op jit(solution)/shard_map/all_to_all | solution.py:57
  28.2 3.9 %all-to-all-start.6 = ((bf16[22,16,88]{2,0,1:T(8,128)(2,1)}), bf16[22,16,88]{2,0,1:T(8,128)(2,1)S(1)}, u32[]{:S(2)}, u32[]{:S(2)}) async-start(bf16[22,16,88]{2,0,1:T(8,128)(2,1)} %copy.100), calls=%async_computation.6 | async-start | bytes 196608 | tf_op jit(solution)/shard_map/all_to_all | solution.py:58
  32.1 0.7 copy.86
  32.8 5.2 %all-to-all-done.6 = bf16[22,16,88]{2,0,1:T(8,128)(2,1)S(1)} async-done(((bf16[22,16,88]{2,0,1:T(8,128)(2,1)}), bf16[22,16,88]{2,0,1:T(8,128)(2,1)S(1)}, u32[]{:S(2)}, u32[]{:S(2)}) %all-to-all-start.6) | async-done | bytes 61984 | tf_op jit(solution)/shard_map/all_to_all | solution.py:58
  38.0 6.6 %all-to-all-start.1 = ((bf16[8,2,22,88]{3,1,2,0:T(2,128)(2,1)}), bf16[8,2,22,88]{3,1,2,0:T(2,128)(2,1)S(1)}, u32[]{:S(2)}, u32[]{:S(2)}) async-start(bf16[8,2,22,88]{3,1,2,0:T(2,128)(2,1)} %copy.86), calls=%async_computation.1 | async-start | bytes 180224 | tf_op jit(solution)/shard_map/all_to_all | solution.py:65
  44.7 0.7 copy.94
  45.4 6.8 %all-to-all-done.1 = bf16[8,2,22,88]{3,1,2,0:T(2,128)(2,1)S(1)} async-done(((bf16[8,2,22,88]{3,1,2,0:T(2,128)(2,1)}), bf16[8,2,22,88]{3,1,2,0:T(2,128)(2,1)S(1)}, u32[]{:S(2)}, u32[]{:S(2)}) %all-to-all-start.1) | async-done | bytes 61984 | tf_op jit(solution)/shard_map/all_to_all | solution.py:65
  52.1 3.4 %all-to-all-start.4 = ((bf16[8,2,22,88]{3,1,2,0:T(2,128)(2,1)}), bf16[8,2,22,88]{3,1,2,0:T(2,128)(2,1)S(1)}, u32[]{:S(2)}, u32[]{:S(2)}) async-start(bf16[8,2,22,88]{3,1,2,0:T(2,128)(2,1)} %copy.94), calls=%async_computation.4 | async-start | bytes 180224 | tf_op jit(solution)/shard_map/all_to_all | solution.py:65
  55.5 0.7 copy.102
  56.2 6.8 %all-to-all-done.4 = bf16[8,2,22,88]{3,1,2,0:T(2,128)(2,1)S(1)} async-done(((bf16[8,2,22,88]{3,1,2,0:T(2,128)(2,1)}), bf16[8,2,22,88]{3,1,2,0:T(2,128)(2,1)S(1)}, u32[]{:S(2)}, u32[]{:S(2)}) %all-to-all-start.4) | async-done | bytes 61984 | tf_op jit(solution)/shard_map/all_to_all | solution.py:65
  63.0 3.4 %all-to-all-start.7 = ((bf16[8,2,22,88]{3,1,2,0:T(2,128)(2,1)}), bf16[8,2,22,88]{3,1,2,0:T(2,128)(2,1)S(1)}, u32[]{:S(2)}, u32[]{:S(2)}) async-start(bf16[8,2,22,88]{3,1,2,0:T(2,128)(2,1)} %copy.102), calls=%async_computation.7 | async-start | bytes 180224 | tf_op jit(solution)/shard_map/all_to_all | solution.py:65
  66.4 0.7 copy.88
  67.1 6.7 %all-to-all-done.7 = bf16[8,2,22,88]{3,1,2,0:T(2,128)(2,1)S(1)} async-done(((bf16[8,2,22,88]{3,1,2,0:T(2,128)(2,1)}), bf16[8,2,22,88]{3,1,2,0:T(2,128)(2,1)S(1)}, u32[]{:S(2)}, u32[]{:S(2)}) %all-to-all-start.7) | async-done | bytes 61984 | tf_op jit(solution)/shard_map/all_to_all | solution.py:65
  73.8 5.9 %all-to-all-start.2 = ((bf16[4,4,1,22,88]{4,1,3,2,0:T(4,128)(2,1)}), bf16[4,4,1,22,88]{4,1,3,2,0:T(4,128)(2,1)S(1)}, u32[]{:S(2)}, u32[]{:S(2)}) async-start(bf16[4,4,1,22,88]{4,1,3,2,0:T(4,128)(2,1)} %copy.88), calls=%async_computation.2 | async-start | bytes 180224 | tf_op jit(solution)/shard_map/all_to_all | solution.py:73
  79.7 0.7 copy.96
  80.4 6.3 %all-to-all-done.2 = bf16[4,4,1,22,88]{4,1,3,2,0:T(4,128)(2,1)S(1)} async-done(((bf16[4,4,1,22,88]{4,1,3,2,0:T(4,128)(2,1)}), bf16[4,4,1,22,88]{4,1,3,2,0:T(4,128)(2,1)S(1)}, u32[]{:S(2)}, u32[]{:S(2)}) %all-to-all-start.2) | async-done | bytes 61984 | tf_op jit(solution)/shard_map/all_to_all | solution.py:73
  86.7 3.3 %all-to-all-start.5 = ((bf16[4,4,1,22,88]{4,1,3,2,0:T(4,128)(2,1)}), bf16[4,4,1,22,88]{4,1,3,2,0:T(4,128)(2,1)S(1)}, u32[]{:S(2)}, u32[]{:S(2)}) async-start(bf16[4,4,1,22,88]{4,1,3,2,0:T(4,128)(2,1)} %copy.96), calls=%async_computation.5 | async-start | bytes 180224 | tf_op jit(solution)/shard_map/all_to_all | solution.py:73
  90.0 0.8 dynamic_slice.3
  90.8 0.7 copy.104
  91.6 0.1 copy.90
  91.7 3.8 %all_gather.27 = bf16[2,352,88]{1,2,0:T(8,128)(2,1)S(1)} all-gather(bf16[1,352,88]{1,2,0:T(8,128)(2,1)S(1)} %copy.90), channel_id=1, replica_groups=mesh['dp_0'=4,'dp_1'=2,'dp_2'=2,'pipe'=8,'tensor'=4] {'dp_1'}, dimensions={0}, use_global_device_ids=true | all-gather | bytes 185856 | tf_op jit(solution)/shard_map/all_gather | solution.py:25
  95.5 1.5 all-to-all-done.5
  97.0 5.1 %all-to-all-start.8 = ((bf16[4,4,1,22,88]{4,1,3,2,0:T(4,128)(2,1)}), bf16[4,4,1,22,88]{4,1,3,2,0:T(4,128)(2,1)S(1)}, u32[]{:S(2)}, u32[]{:S(2)}) async-start(bf16[4,4,1,22,88]{4,1,3,2,0:T(4,128)(2,1)} %copy.104), calls=%async_computation.8 | async-start | bytes 180224 | tf_op jit(solution)/shard_map/all_to_all | solution.py:73
  102.1 0.1 copy.98
  102.3 4.3 %all_gather.30 = bf16[2,352,88]{1,2,0:T(8,128)(2,1)S(1)} all-gather(bf16[1,352,88]{1,2,0:T(8,128)(2,1)S(1)} %copy.98), channel_id=1, replica_groups=mesh['dp_0'=4,'dp_1'=2,'dp_2'=2,'pipe'=8,'tensor'=4] {'dp_1'}, dimensions={0}, use_global_device_ids=true | all-gather | bytes 185856 | tf_op jit(solution)/shard_map/all_gather | solution.py:25
  106.5 10.5 %all_gather.31 = bf16[8,352,88]{1,2,0:T(8,128)(2,1)S(1)} all-gather(bf16[2,352,88]{1,2,0:T(8,128)(2,1)S(1)} %all_gather.30), channel_id=1, replica_groups=mesh['dp_0'=4,'dp_1'=2,'dp_2'=2,'pipe'=8,'tensor'=4] {'dp_0'}, dimensions={0}, use_global_device_ids=true | all-gather | bytes 619520 | tf_op jit(solution)/shard_map/all_gather | solution.py:25
  117.1 11.4 %all_gather.28 = bf16[8,352,88]{1,2,0:T(8,128)(2,1)S(1)} all-gather(bf16[2,352,88]{1,2,0:T(8,128)(2,1)S(1)} %all_gather.27), channel_id=1, replica_groups=mesh['dp_0'=4,'dp_1'=2,'dp_2'=2,'pipe'=8,'tensor'=4] {'dp_0'}, dimensions={0}, use_global_device_ids=true | all-gather | bytes 619520 | tf_op jit(solution)/shard_map/all_gather | solution.py:25
  128.4 15.4 %all_gather.29 = bf16[16,352,88]{1,2,0:T(8,128)(2,1)S(1)} all-gather(bf16[8,352,88]{1,2,0:T(8,128)(2,1)S(1)} %all_gather.28), channel_id=1, replica_groups=mesh['dp_0'=4,'dp_1'=2,'dp_2'=2,'pipe'=8,'tensor'=4] {'dp_2'}, dimensions={0}, use_global_device_ids=true | all-gather | bytes 1486848 | tf_op jit(solution)/shard_map/all_gather | solution.py:25
  143.8 0.1 copy.91
  143.9 1.9 %copy.108 = bf16[352,1408]{1,0:T(8,128)(2,1)} copy(bf16[352,1408]{0,1:T(8,128)(2,1)S(1)} %bitcast.77) | data formatting | bytes 1982464
  145.8 1.0 convolution_reduce_fusion.2
  146.8 2.6 %all_gather.32 = bf16[16,352,88]{1,2,0:T(8,128)(2,1)S(1)} all-gather(bf16[8,352,88]{1,2,0:T(8,128)(2,1)S(1)} %all_gather.31), channel_id=1, replica_groups=mesh['dp_0'=4,'dp_1'=2,'dp_2'=2,'pipe'=8,'tensor'=4] {'dp_2'}, dimensions={0}, use_global_device_ids=true | all-gather | bytes 1486848 | tf_op jit(solution)/shard_map/all_gather | solution.py:25
  149.4 0.1 copy.99
  149.5 1.9 %copy.109 = bf16[352,1408]{1,0:T(8,128)(2,1)} copy(bf16[352,1408]{0,1:T(8,128)(2,1)S(1)} %bitcast.79) | data formatting | bytes 1982464
  151.4 1.0 convolution_reduce_fusion.1
  152.4 0.0 all-to-all-done.8
  152.5 0.1 copy.106
  152.6 3.8 %all_gather.33 = bf16[2,352,88]{1,2,0:T(8,128)(2,1)S(1)} all-gather(bf16[1,352,88]{1,2,0:T(8,128)(2,1)S(1)} %copy.106), channel_id=1, replica_groups=mesh['dp_0'=4,'dp_1'=2,'dp_2'=2,'pipe'=8,'tensor'=4] {'dp_1'}, dimensions={0}, use_global_device_ids=true | all-gather | bytes 185856 | tf_op jit(solution)/shard_map/all_gather | solution.py:25
  156.4 10.2 %all_gather.34 = bf16[8,352,88]{1,2,0:T(8,128)(2,1)S(1)} all-gather(bf16[2,352,88]{1,2,0:T(8,128)(2,1)S(1)} %all_gather.33), channel_id=1, replica_groups=mesh['dp_0'=4,'dp_1'=2,'dp_2'=2,'pipe'=8,'tensor'=4] {'dp_0'}, dimensions={0}, use_global_device_ids=true | all-gather | bytes 619520 | tf_op jit(solution)/shard_map/all_gather | solution.py:25
  166.6 6.7 %all_gather.35 = bf16[16,352,88]{1,2,0:T(8,128)(2,1)S(1)} all-gather(bf16[8,352,88]{1,2,0:T(8,128)(2,1)S(1)} %all_gather.34), channel_id=1, replica_groups=mesh['dp_0'=4,'dp_1'=2,'dp_2'=2,'pipe'=8,'tensor'=4] {'dp_2'}, dimensions={0}, use_global_device_ids=true | all-gather | bytes 1486848 | tf_op jit(solution)/shard_map/all_gather | solution.py:25
  173.3 0.1 copy.107
  173.4 1.0 convolution_reduce_fusion
  174.4 0.0 copy-start.1
  174.4 1.9 %copy.110 = bf16[352,1408]{1,0:T(8,128)(2,1)} copy(bf16[352,1408]{0,1:T(8,128)(2,1)S(1)} %bitcast.76) | data formatting | bytes 1982464
  176.3 0.0 copy-done.1
  176.3 0.1 bitcast_reduce_fusion.2
  176.5 0.6 maximum_multiply_fusion
  (13 shorter events, 0.3 us)
Async XLA Ops:
  0.6 21.7 %copy-start = (bf16[22,1408]{1,0:T(8,128)(2,1)S(1)}, bf16[22,1408]{1,0:T(8,128)(2,1)}, u32[]{:S(2)}) copy-start(bf16[22,1408]{1,0:T(8,128)(2,1)} %param.7) | copy-start | bytes 185860
  2.4 16.0 %all-to-all-start = ((bf16[22,16,88]{2,0,1:T(8,128)(2,1)}), bf16[22,16,88]{2,0,1:T(8,128)(2,1)S(1)}, u32[]{:S(2)}, u32[]{:S(2)}) async-start(bf16[22,16,88]{2,0,1:T(8,128)(2,1)} %copy.84), calls=%async_computation | async-start | bytes 196608 | tf_op jit(solution)/shard_map/all_to_all | solution.py:56
  18.4 9.8 %all-to-all-start.3 = ((bf16[22,16,88]{2,0,1:T(8,128)(2,1)}), bf16[22,16,88]{2,0,1:T(8,128)(2,1)S(1)}, u32[]{:S(2)}, u32[]{:S(2)}) async-start(bf16[22,16,88]{2,0,1:T(8,128)(2,1)} %copy.92), calls=%async_computation.3 | async-start | bytes 196608 | tf_op jit(solution)/shard_map/all_to_all | solution.py:57
  28.2 9.8 %all-to-all-start.6 = ((bf16[22,16,88]{2,0,1:T(8,128)(2,1)}), bf16[22,16,88]{2,0,1:T(8,128)(2,1)S(1)}, u32[]{:S(2)}, u32[]{:S(2)}) async-start(bf16[22,16,88]{2,0,1:T(8,128)(2,1)} %copy.100), calls=%async_computation.6 | async-start | bytes 196608 | tf_op jit(solution)/shard_map/all_to_all | solution.py:58
  38.0 14.1 %all-to-all-start.1 = ((bf16[8,2,22,88]{3,1,2,0:T(2,128)(2,1)}), bf16[8,2,22,88]{3,1,2,0:T(2,128)(2,1)S(1)}, u32[]{:S(2)}, u32[]{:S(2)}) async-start(bf16[8,2,22,88]{3,1,2,0:T(2,128)(2,1)} %copy.86), calls=%async_computation.1 | async-start | bytes 180224 | tf_op jit(solution)/shard_map/all_to_all | solution.py:65
  52.1 10.9 %all-to-all-start.4 = ((bf16[8,2,22,88]{3,1,2,0:T(2,128)(2,1)}), bf16[8,2,22,88]{3,1,2,0:T(2,128)(2,1)S(1)}, u32[]{:S(2)}, u32[]{:S(2)}) async-start(bf16[8,2,22,88]{3,1,2,0:T(2,128)(2,1)} %copy.94), calls=%async_computation.4 | async-start | bytes 180224 | tf_op jit(solution)/shard_map/all_to_all | solution.py:65
  63.0 10.8 %all-to-all-start.7 = ((bf16[8,2,22,88]{3,1,2,0:T(2,128)(2,1)}), bf16[8,2,22,88]{3,1,2,0:T(2,128)(2,1)S(1)}, u32[]{:S(2)}, u32[]{:S(2)}) async-start(bf16[8,2,22,88]{3,1,2,0:T(2,128)(2,1)} %copy.102), calls=%async_computation.7 | async-start | bytes 180224 | tf_op jit(solution)/shard_map/all_to_all | solution.py:65
  73.8 12.9 %all-to-all-start.2 = ((bf16[4,4,1,22,88]{4,1,3,2,0:T(4,128)(2,1)}), bf16[4,4,1,22,88]{4,1,3,2,0:T(4,128)(2,1)S(1)}, u32[]{:S(2)}, u32[]{:S(2)}) async-start(bf16[4,4,1,22,88]{4,1,3,2,0:T(4,128)(2,1)} %copy.88), calls=%async_computation.2 | async-start | bytes 180224 | tf_op jit(solution)/shard_map/all_to_all | solution.py:73
  86.7 10.3 %all-to-all-start.5 = ((bf16[4,4,1,22,88]{4,1,3,2,0:T(4,128)(2,1)}), bf16[4,4,1,22,88]{4,1,3,2,0:T(4,128)(2,1)S(1)}, u32[]{:S(2)}, u32[]{:S(2)}) async-start(bf16[4,4,1,22,88]{4,1,3,2,0:T(4,128)(2,1)} %copy.96), calls=%async_computation.5 | async-start | bytes 180224 | tf_op jit(solution)/shard_map/all_to_all | solution.py:73
  97.0 55.4 %all-to-all-start.8 = ((bf16[4,4,1,22,88]{4,1,3,2,0:T(4,128)(2,1)}), bf16[4,4,1,22,88]{4,1,3,2,0:T(4,128)(2,1)S(1)}, u32[]{:S(2)}, u32[]{:S(2)}) async-start(bf16[4,4,1,22,88]{4,1,3,2,0:T(4,128)(2,1)} %copy.104), calls=%async_computation.8 | async-start | bytes 180224 | tf_op jit(solution)/shard_map/all_to_all | solution.py:73
  174.4 1.9 %copy-start.1 = (f32[1408]{0:T(1024)S(1)}, f32[1408]{0:T(1024)}, u32[]{:S(2)}) copy-start(f32[1408]{0:T(1024)} %param.9) | copy-start | bytes 16900
where the time goes:
time: 178 us; the launch traced here: 177 us
  blocking collectives  68.7 us (39%)
  starting transfers between devices  45.5 us (26%)
  waiting for transfers between devices  42.5 us (24%)
  local copies, waits for them, and re-layouts  15.8 us (9%)
  matrix products  2.99 us (2%)
    all_gather x9, blocking collectives, gather_in_order(): blocks = lax.all_gather(blocks, axes[k], axis=0, tiled=True)  68.7 us
    all_to_all x3, waiting for transfers between devices, shards(): lax.all_to_all(for_sending(grouped), 'pipe', split_axis=0, concat_axis=2,...  20.2 us
    all_to_all x3, starting transfers between devices, shards(): lax.all_to_all(for_sending(routed), 'tensor', split_axis=0, concat_axis=2...  14.3 us
    all_to_all x3, starting transfers between devices, shards(): lax.all_to_all(for_sending(grouped), 'pipe', split_axis=0, concat_axis=2,...  13.4 us
    all_to_all x1, starting transfers between devices, shards(): lax.all_to_all(sources[0], DP, split_axis=1, concat_axis=0, tiled=True)  10.1 us
    all_to_all x3, waiting for transfers between devices, shards(): lax.all_to_all(for_sending(routed), 'tensor', split_axis=0, concat_axis=2...  7.87 us
    unnamed x7, local copies, waits for them, and re-layouts  5.68 us
    all_to_all x1, waiting for transfers between devices, shards(): lax.all_to_all(sources[2], DP, split_axis=1, concat_axis=0, tiled=True)  5.18 us
  transfers between devices with their start and end apart: 9, of which 8 were waited for; matrix products, arithmetic and copies ran while one was open for 7% of the time, Pallas kernels for 0%

commit v1 on v0

--- a/solution.py
+++ b/solution.py
@@ -22,7 +22,8 @@
 def gather_in_order(array, axes, order):
     blocks = array[None]
     for k in order:
-        blocks = lax.all_gather(blocks, axes[k], axis=0, tiled=True)
+        repeated = jnp.stack([blocks] * lax.axis_size(axes[k]))
+        blocks = jnp.concatenate(lax.all_to_all(repeated, axes[k], 0, 0), axis=0)
     block = [lax.axis_size(axes[k]) for k in reversed(order)]
     blocks = blocks.reshape(*block, *array.shape)
     turned = sorted(range(len(order)), key=lambda place: order[len(order) - 1 - place])

time: 178 us -> 200 us (1.12)
  waiting for transfers between devices: 42.5 us -> 70.3 us
  blocking collectives: 68.7 us -> 43.5 us
  starting transfers between devices: 45.5 us -> 58.2 us
  local copies, waits for them, and re-layouts: 15.8 us -> 19 us
  other arithmetic: 0.72 us -> 3.67 us
    all_gather x9 -> x0, blocking collectives: 68.7 us -> none  [gather_in_order(): blocks = lax.all_gather(blocks, axes[k], axis=0, tiled=True)]
    all_to_all x0 -> x5, blocking collectives: none -> 43.5 us  [gather_in_order(): blocks = jnp.concatenate(lax.all_to_all(repeated, axes[k], 0, 0), axis=0)]
    all_to_all x0 -> x4, waiting for transfers between devices: none -> 17 us  [gather_in_order(): blocks = jnp.concatenate(lax.all_to_all(repeated, axes[k], 0, 0), axis=0)]
    all_to_all x0 -> x4, starting transfers between devices: none -> 14.5 us  [gather_in_order(): blocks = jnp.concatenate(lax.all_to_all(repeated, axes[k], 0, 0), axis=0)]
    all_to_all x3, waiting for transfers between devices: 7.87 us -> 18.7 us  [shards(): lax.all_to_all(for_sending(routed), 'tensor', split_axis=0, concat_axis=2...]
    another operation x6 -> x9, local copies, waits for them, and re-layouts: 0.43 us -> 3.58 us  [gather_in_order(): repeated = jnp.stack([blocks] * lax.axis_size(axes[k]))]
    another operation x0 -> x6, other arithmetic: none -> 2.95 us  [gather_in_order(): repeated = jnp.stack([blocks] * lax.axis_size(axes[k]))]
    unnamed x7 -> x9, local copies, waits for them, and re-layouts: 5.68 us -> 5.68 us
  transfers between devices with their start and end apart: 9 -> 13, of which waited for: 8 -> 13; matrix products, arithmetic and copies ran while one was open for 7% -> 8% of each run, Pallas kernels for 0% -> 0%
where the time goes in v1:
time: 200 us; the launch traced here: 199 us
  waiting for transfers between devices  70.3 us (35%)
  starting transfers between devices  58.2 us (29%)
  blocking collectives  43.5 us (22%)
  local copies, waits for them, and re-layouts  19 us (10%)
  other arithmetic  3.67 us (2%)
  matrix products  2.99 us (1%)
    all_to_all x5, blocking collectives, gather_in_order(): blocks = jnp.concatenate(lax.all_to_all(repeated, axes[k], 0, 0), axis=0)  43.5 us
    all_to_all x3, waiting for transfers between devices, shards(): lax.all_to_all(for_sending(grouped), 'pipe', split_axis=0, concat_axis=2,...  20.2 us
    all_to_all x3, waiting for transfers between devices, shards(): lax.all_to_all(for_sending(routed), 'tensor', split_axis=0, concat_axis=2...  18.7 us
    all_to_all x4, waiting for transfers between devices, gather_in_order(): blocks = jnp.concatenate(lax.all_to_all(repeated, axes[k], 0, 0), axis=0)  17 us
    all_to_all x4, starting transfers between devices, gather_in_order(): blocks = jnp.concatenate(lax.all_to_all(repeated, axes[k], 0, 0), axis=0)  14.5 us
    all_to_all x3, starting transfers between devices, shards(): lax.all_to_all(for_sending(grouped), 'pipe', split_axis=0, concat_axis=2,...  13.4 us
    all_to_all x3, starting transfers between devices, shards(): lax.all_to_all(for_sending(routed), 'tensor', split_axis=0, concat_axis=2...  12.5 us
    all_to_all x1, starting transfers between devices, shards(): lax.all_to_all(sources[0], DP, split_axis=1, concat_axis=0, tiled=True)  10.1 us
  transfers between devices with their start and end apart: 13, of which 13 were waited for; matrix products, arithmetic and copies ran while one was open for 8% of the time, Pallas kernels for 0%

profile of v1, /device:TPU:1, one launch (start us, length us, event | category | flops | bytes accessed | tf_op | source)
XLA Modules:
  0.0 198.5 jit_solution(13129834600835587658)
XLA Ops:
  0.6 0.0 copy-start.1
  0.6 1.1 all_to_all.129
  1.7 0.7 copy.87
  2.4 10.1 %all-to-all-start = ((bf16[22,16,88]{2,0,1:T(8,128)(2,1)}), bf16[22,16,88]{2,0,1:T(8,128)(2,1)S(1)}, u32[]{:S(2)}, u32[]{:S(2)}) async-start(bf16[22,16,88]{2,0,1:T(8,128)(2,1)} %copy.87), calls=%async_computation | async-start | bytes 196608 | tf_op jit(solution)/shard_map/all_to_all | solution.py:57
  12.5 1.1 all_to_all.141
  13.6 0.7 copy.95
  14.3 4.2 %all-to-all-done = bf16[22,16,88]{2,0,1:T(8,128)(2,1)S(1)} async-done(((bf16[22,16,88]{2,0,1:T(8,128)(2,1)}), bf16[22,16,88]{2,0,1:T(8,128)(2,1)S(1)}, u32[]{:S(2)}, u32[]{:S(2)}) %all-to-all-start) | async-done | bytes 61984 | tf_op jit(solution)/shard_map/all_to_all | solution.py:57
  18.4 3.9 %all-to-all-start.6 = ((bf16[22,16,88]{2,0,1:T(8,128)(2,1)}), bf16[22,16,88]{2,0,1:T(8,128)(2,1)S(1)}, u32[]{:S(2)}, u32[]{:S(2)}) async-start(bf16[22,16,88]{2,0,1:T(8,128)(2,1)} %copy.95), calls=%async_computation.6 | async-start | bytes 196608 | tf_op jit(solution)/shard_map/all_to_all | solution.py:58
  22.3 0.2 all_to_all.153
  22.5 0.7 copy.103
  23.2 5.0 %all-to-all-done.6 = bf16[22,16,88]{2,0,1:T(8,128)(2,1)S(1)} async-done(((bf16[22,16,88]{2,0,1:T(8,128)(2,1)}), bf16[22,16,88]{2,0,1:T(8,128)(2,1)S(1)}, u32[]{:S(2)}, u32[]{:S(2)}) %all-to-all-start.6) | async-done | bytes 61984 | tf_op jit(solution)/shard_map/all_to_all | solution.py:58
  28.2 3.9 %all-to-all-start.12 = ((bf16[22,16,88]{2,0,1:T(8,128)(2,1)}), bf16[22,16,88]{2,0,1:T(8,128)(2,1)S(1)}, u32[]{:S(2)}, u32[]{:S(2)}) async-start(bf16[22,16,88]{2,0,1:T(8,128)(2,1)} %copy.103), calls=%async_computation.12 | async-start | bytes 196608 | tf_op jit(solution)/shard_map/all_to_all | solution.py:59
  32.1 0.7 copy.89
  32.8 5.2 %all-to-all-done.12 = bf16[22,16,88]{2,0,1:T(8,128)(2,1)S(1)} async-done(((bf16[22,16,88]{2,0,1:T(8,128)(2,1)}), bf16[22,16,88]{2,0,1:T(8,128)(2,1)S(1)}, u32[]{:S(2)}, u32[]{:S(2)}) %all-to-all-start.12) | async-done | bytes 61984 | tf_op jit(solution)/shard_map/all_to_all | solution.py:59
  38.0 6.6 %all-to-all-start.1 = ((bf16[8,2,22,88]{3,1,2,0:T(2,128)(2,1)}), bf16[8,2,22,88]{3,1,2,0:T(2,128)(2,1)S(1)}, u32[]{:S(2)}, u32[]{:S(2)}) async-start(bf16[8,2,22,88]{3,1,2,0:T(2,128)(2,1)} %copy.89), calls=%async_computation.1 | async-start | bytes 180224 | tf_op jit(solution)/shard_map/all_to_all | solution.py:66
  44.7 0.7 copy.97
  45.4 6.8 %all-to-all-done.1 = bf16[8,2,22,88]{3,1,2,0:T(2,128)(2,1)S(1)} async-done(((bf16[8,2,22,88]{3,1,2,0:T(2,128)(2,1)}), bf16[8,2,22,88]{3,1,2,0:T(2,128)(2,1)S(1)}, u32[]{:S(2)}, u32[]{:S(2)}) %all-to-all-start.1) | async-done | bytes 61984 | tf_op jit(solution)/shard_map/all_to_all | solution.py:66
  52.1 3.4 %all-to-all-start.7 = ((bf16[8,2,22,88]{3,1,2,0:T(2,128)(2,1)}), bf16[8,2,22,88]{3,1,2,0:T(2,128)(2,1)S(1)}, u32[]{:S(2)}, u32[]{:S(2)}) async-start(bf16[8,2,22,88]{3,1,2,0:T(2,128)(2,1)} %copy.97), calls=%async_computation.7 | async-start | bytes 180224 | tf_op jit(solution)/shard_map/all_to_all | solution.py:66
  55.5 0.7 copy.105
  56.2 6.8 %all-to-all-done.7 = bf16[8,2,22,88]{3,1,2,0:T(2,128)(2,1)S(1)} async-done(((bf16[8,2,22,88]{3,1,2,0:T(2,128)(2,1)}), bf16[8,2,22,88]{3,1,2,0:T(2,128)(2,1)S(1)}, u32[]{:S(2)}, u32[]{:S(2)}) %all-to-all-start.7) | async-done | bytes 61984 | tf_op jit(solution)/shard_map/all_to_all | solution.py:66
  63.0 3.4 %all-to-all-start.13 = ((bf16[8,2,22,88]{3,1,2,0:T(2,128)(2,1)}), bf16[8,2,22,88]{3,1,2,0:T(2,128)(2,1)S(1)}, u32[]{:S(2)}, u32[]{:S(2)}) async-start(bf16[8,2,22,88]{3,1,2,0:T(2,128)(2,1)} %copy.105), calls=%async_computation.13 | async-start | bytes 180224 | tf_op jit(solution)/shard_map/all_to_all | solution.py:66
  66.4 0.7 copy.91
  67.1 6.7 %all-to-all-done.13 = bf16[8,2,22,88]{3,1,2,0:T(2,128)(2,1)S(1)} async-done(((bf16[8,2,22,88]{3,1,2,0:T(2,128)(2,1)}), bf16[8,2,22,88]{3,1,2,0:T(2,128)(2,1)S(1)}, u32[]{:S(2)}, u32[]{:S(2)}) %all-to-all-start.13) | async-done | bytes 61984 | tf_op jit(solution)/shard_map/all_to_all | solution.py:66
  73.8 5.9 %all-to-all-start.2 = ((bf16[4,4,1,22,88]{4,1,3,2,0:T(4,128)(2,1)}), bf16[4,4,1,22,88]{4,1,3,2,0:T(4,128)(2,1)S(1)}, u32[]{:S(2)}, u32[]{:S(2)}) async-start(bf16[4,4,1,22,88]{4,1,3,2,0:T(4,128)(2,1)} %copy.91), calls=%async_computation.2 | async-start | bytes 180224 | tf_op jit(solution)/shard_map/all_to_all | solution.py:74
  79.7 0.7 copy.99
  80.4 6.3 %all-to-all-done.2 = bf16[4,4,1,22,88]{4,1,3,2,0:T(4,128)(2,1)S(1)} async-done(((bf16[4,4,1,22,88]{4,1,3,2,0:T(4,128)(2,1)}), bf16[4,4,1,22,88]{4,1,3,2,0:T(4,128)(2,1)S(1)}, u32[]{:S(2)}, u32[]{:S(2)}) %all-to-all-start.2) | async-done | bytes 61984 | tf_op jit(solution)/shard_map/all_to_all | solution.py:74
  86.7 3.3 %all-to-all-start.8 = ((bf16[4,4,1,22,88]{4,1,3,2,0:T(4,128)(2,1)}), bf16[4,4,1,22,88]{4,1,3,2,0:T(4,128)(2,1)S(1)}, u32[]{:S(2)}, u32[]{:S(2)}) async-start(bf16[4,4,1,22,88]{4,1,3,2,0:T(4,128)(2,1)} %copy.99), calls=%async_computation.8 | async-start | bytes 180224 | tf_op jit(solution)/shard_map/all_to_all | solution.py:74
  90.1 0.7 copy.107
  90.8 6.2 %all-to-all-done.8 = bf16[4,4,1,22,88]{4,1,3,2,0:T(4,128)(2,1)S(1)} async-done(((bf16[4,4,1,22,88]{4,1,3,2,0:T(4,128)(2,1)}), bf16[4,4,1,22,88]{4,1,3,2,0:T(4,128)(2,1)S(1)}, u32[]{:S(2)}, u32[]{:S(2)}) %all-to-all-start.8) | async-done | bytes 61984 | tf_op jit(solution)/shard_map/all_to_all | solution.py:74
  97.0 3.3 %all-to-all-start.14 = ((bf16[4,4,1,22,88]{4,1,3,2,0:T(4,128)(2,1)}), bf16[4,4,1,22,88]{4,1,3,2,0:T(4,128)(2,1)S(1)}, u32[]{:S(2)}, u32[]{:S(2)}) async-start(bf16[4,4,1,22,88]{4,1,3,2,0:T(4,128)(2,1)} %copy.107), calls=%async_computation.14 | async-start | bytes 180224 | tf_op jit(solution)/shard_map/all_to_all | solution.py:74
  100.4 0.8 copy.93
  101.2 6.1 %all-to-all-done.14 = bf16[4,4,1,22,88]{4,1,3,2,0:T(4,128)(2,1)S(1)} async-done(((bf16[4,4,1,22,88]{4,1,3,2,0:T(4,128)(2,1)}), bf16[4,4,1,22,88]{4,1,3,2,0:T(4,128)(2,1)S(1)}, u32[]{:S(2)}, u32[]{:S(2)}) %all-to-all-start.14) | async-done | bytes 61984 | tf_op jit(solution)/shard_map/all_to_all | solution.py:74
  107.3 3.4 %all-to-all-start.3 = ((bf16[2,1,352,88]{2,3,1,0:T(8,128)(2,1)}), bf16[2,1,352,88]{2,3,1,0:T(8,128)(2,1)S(1)}, u32[]{:S(2)}, u32[]{:S(2)}) async-start(bf16[2,1,352,88]{2,3,1,0:T(8,128)(2,1)} %copy.93), calls=%async_computation.3 | async-start | bytes 270336 | tf_op jit(solution)/shard_map/all_to_all | solution.py:26
  110.9 0.1 copy.101
  111.0 3.4 %all-to-all-done.3 = bf16[2,1,352,88]{2,3,1,0:T(8,128)(2,1)S(1)} async-done(((bf16[2,1,352,88]{2,3,1,0:T(8,128)(2,1)}), bf16[2,1,352,88]{2,3,1,0:T(8,128)(2,1)S(1)}, u32[]{:S(2)}, u32[]{:S(2)}) %all-to-all-start.3) | async-done | bytes 123936 | tf_op jit(solution)/shard_map/all_to_all | solution.py:26
  114.4 5.7 %all_to_all.183 = bf16[2,1,352,88]{2,3,1,0:T(8,128)(2,1)S(1)} all-to-all(bf16[2,1,352,88]{2,3,1,0:T(8,128)(2,1)S(1)} %copy.101), channel_id=1, replica_groups=mesh['dp_0'=4,'dp_1'=2,'dp_2'=2,'pipe'=8,'tensor'=4] {'dp_1'}, dimensions={0} | all-to-all | bytes 247808 | tf_op jit(solution)/shard_map/all_to_all | solution.py:26
  120.1 9.4 %all_to_all.184 = bf16[4,2,352,88]{2,3,1,0:T(8,128)(2,1)S(1)} all-to-all(bf16[4,2,352,88]{2,3,1,0:T(8,128)(2,1)S(1)} %stack.40), channel_id=1, replica_groups=mesh['dp_0'=4,'dp_1'=2,'dp_2'=2,'pipe'=8,'tensor'=4] {'dp_0'}, dimensions={0} | all-to-all | bytes 991232 | tf_op jit(solution)/shard_map/all_to_all | solution.py:26
  129.5 0.8 stack.43
  130.4 3.5 %all-to-all-start.10 = ((bf16[4,2,352,88]{2,3,1,0:T(8,128)(2,1)}), bf16[4,2,352,88]{2,3,1,0:T(8,128)(2,1)S(1)}, u32[]{:S(2)}, u32[]{:S(2)}) async-start(bf16[4,2,352,88]{2,3,1,0:T(8,128)(2,1)} %stack.43), calls=%async_computation.10 | async-start | bytes 1081344 | tf_op jit(solution)/shard_map/all_to_all | solution.py:26
  134.0 0.8 copy.109
  134.8 0.2 pad_maximum_fusion
  135.0 8.8 %all-to-all-done.10 = bf16[4,2,352,88]{2,3,1,0:T(8,128)(2,1)S(1)} async-done(((bf16[4,2,352,88]{2,3,1,0:T(8,128)(2,1)}), bf16[4,2,352,88]{2,3,1,0:T(8,128)(2,1)S(1)}, u32[]{:S(2)}, u32[]{:S(2)}) %all-to-all-start.10) | async-done | bytes 495648 | tf_op jit(solution)/shard_map/all_to_all | solution.py:26
  143.8 3.4 %all-to-all-start.15 = ((bf16[2,1,352,88]{2,3,1,0:T(8,128)(2,1)}), bf16[2,1,352,88]{2,3,1,0:T(8,128)(2,1)S(1)}, u32[]{:S(2)}, u32[]{:S(2)}) async-start(bf16[2,1,352,88]{2,3,1,0:T(8,128)(2,1)} %copy.109), calls=%async_computation.15 | async-start | bytes 270336 | tf_op jit(solution)/shard_map/all_to_all | solution.py:26
  147.2 1.2 pad_maximum_fusion.1
  148.4 2.1 %all-to-all-done.15 = bf16[2,1,352,88]{2,3,1,0:T(8,128)(2,1)S(1)} async-done(((bf16[2,1,352,88]{2,3,1,0:T(8,128)(2,1)}), bf16[2,1,352,88]{2,3,1,0:T(8,128)(2,1)S(1)}, u32[]{:S(2)}, u32[]{:S(2)}) %all-to-all-start.15) | async-done | bytes 123936 | tf_op jit(solution)/shard_map/all_to_all | solution.py:26
  150.6 18.3 %all_to_all.185 = bf16[2,8,352,88]{2,3,1,0:T(8,128)(2,1)S(1)} all-to-all(bf16[2,8,352,88]{2,3,1,0:T(8,128)(2,1)S(1)} %pad_maximum_fusion), channel_id=1, replica_groups=mesh['dp_0'=4,'dp_1'=2,'dp_2'=2,'pipe'=8,'tensor'=4] {'dp_2'}, dimensions={0} | all-to-all | bytes 1982464 | tf_op jit(solution)/shard_map/all_to_all | solution.py:26
  168.9 4.6 %all_to_all.186 = bf16[2,8,352,88]{2,3,1,0:T(8,128)(2,1)S(1)} all-to-all(bf16[2,8,352,88]{2,3,1,0:T(8,128)(2,1)S(1)} %copy-done), channel_id=1, replica_groups=mesh['dp_0'=4,'dp_1'=2,'dp_2'=2,'pipe'=8,'tensor'=4] {'dp_2'}, dimensions={0} | all-to-all | bytes 1982464 | tf_op jit(solution)/shard_map/all_to_all | solution.py:26
  173.5 0.8 stack.46
  174.3 4.2 %all-to-all-start.16 = ((bf16[4,2,352,88]{2,3,1,0:T(8,128)(2,1)}), bf16[4,2,352,88]{2,3,1,0:T(8,128)(2,1)}, u32[]{:S(2)}, u32[]{:S(2)}) async-start(bf16[4,2,352,88]{2,3,1,0:T(8,128)(2,1)} %stack.46), calls=%async_computation.16 | async-start | bytes 1081344 | tf_op jit(solution)/shard_map/all_to_all | solution.py:26
  178.5 0.8 dynamic_slice.3
  179.3 0.1 copy.94
  179.4 1.9 copy.111
  181.3 0.1 copy.102
  181.4 1.9 copy.112
  183.3 1.0 convolution_reduce_fusion.2
  184.3 1.0 convolution_reduce_fusion.1
  185.3 2.6 %all-to-all-done.16 = bf16[4,2,352,88]{2,3,1,0:T(8,128)(2,1)} async-done(((bf16[4,2,352,88]{2,3,1,0:T(8,128)(2,1)}), bf16[4,2,352,88]{2,3,1,0:T(8,128)(2,1)}, u32[]{:S(2)}, u32[]{:S(2)}) %all-to-all-start.16) | async-done | bytes 495648 | tf_op jit(solution)/shard_map/all_to_all | solution.py:26
  187.9 1.4 pad_maximum_fusion.2
  189.3 5.4 %all_to_all.187 = bf16[2,8,352,88]{2,3,1,0:T(8,128)(2,1)S(1)} all-to-all(bf16[2,8,352,88]{2,3,1,0:T(8,128)(2,1)S(1)} %pad_maximum_fusion.2), channel_id=1, replica_groups=mesh['dp_0'=4,'dp_1'=2,'dp_2'=2,'pipe'=8,'tensor'=4] {'dp_2'}, dimensions={0} | all-to-all | bytes 1982464 | tf_op jit(solution)/shard_map/all_to_all | solution.py:26
  194.8 0.1 copy.110
  194.9 1.0 convolution_reduce_fusion
  195.9 1.9 copy.113
  197.8 0.1 bitcast_reduce_fusion.2
  197.9 0.6 maximum_multiply_fusion
  (22 shorter events, 0.4 us)
Async XLA Ops:
  0.6 21.7 %copy-start.1 = (bf16[22,1408]{1,0:T(8,128)(2,1)S(1)}, bf16[22,1408]{1,0:T(8,128)(2,1)}, u32[]{:S(2)}) copy-start(bf16[22,1408]{1,0:T(8,128)(2,1)} %param.7) | copy-start | bytes 185860
  2.4 16.0 %all-to-all-start = ((bf16[22,16,88]{2,0,1:T(8,128)(2,1)}), bf16[22,16,88]{2,0,1:T(8,128)(2,1)S(1)}, u32[]{:S(2)}, u32[]{:S(2)}) async-start(bf16[22,16,88]{2,0,1:T(8,128)(2,1)} %copy.87), calls=%async_computation | async-start | bytes 196608 | tf_op jit(solution)/shard_map/all_to_all | solution.py:57
  18.4 9.8 %all-to-all-start.6 = ((bf16[22,16,88]{2,0,1:T(8,128)(2,1)}), bf16[22,16,88]{2,0,1:T(8,128)(2,1)S(1)}, u32[]{:S(2)}, u32[]{:S(2)}) async-start(bf16[22,16,88]{2,0,1:T(8,128)(2,1)} %copy.95), calls=%async_computation.6 | async-start | bytes 196608 | tf_op jit(solution)/shard_map/all_to_all | solution.py:58
  28.2 9.8 %all-to-all-start.12 = ((bf16[22,16,88]{2,0,1:T(8,128)(2,1)}), bf16[22,16,88]{2,0,1:T(8,128)(2,1)S(1)}, u32[]{:S(2)}, u32[]{:S(2)}) async-start(bf16[22,16,88]{2,0,1:T(8,128)(2,1)} %copy.103), calls=%async_computation.12 | async-start | bytes 196608 | tf_op jit(solution)/shard_map/all_to_all | solution.py:59
  38.0 14.1 %all-to-all-start.1 = ((bf16[8,2,22,88]{3,1,2,0:T(2,128)(2,1)}), bf16[8,2,22,88]{3,1,2,0:T(2,128)(2,1)S(1)}, u32[]{:S(2)}, u32[]{:S(2)}) async-start(bf16[8,2,22,88]{3,1,2,0:T(2,128)(2,1)} %copy.89), calls=%async_computation.1 | async-start | bytes 180224 | tf_op jit(solution)/shard_map/all_to_all | solution.py:66
  52.1 10.9 %all-to-all-start.7 = ((bf16[8,2,22,88]{3,1,2,0:T(2,128)(2,1)}), bf16[8,2,22,88]{3,1,2,0:T(2,128)(2,1)S(1)}, u32[]{:S(2)}, u32[]{:S(2)}) async-start(bf16[8,2,22,88]{3,1,2,0:T(2,128)(2,1)} %copy.97), calls=%async_computation.7 | async-start | bytes 180224 | tf_op jit(solution)/shard_map/all_to_all | solution.py:66
  63.0 10.8 %all-to-all-start.13 = ((bf16[8,2,22,88]{3,1,2,0:T(2,128)(2,1)}), bf16[8,2,22,88]{3,1,2,0:T(2,128)(2,1)S(1)}, u32[]{:S(2)}, u32[]{:S(2)}) async-start(bf16[8,2,22,88]{3,1,2,0:T(2,128)(2,1)} %copy.105), calls=%async_computation.13 | async-start | bytes 180224 | tf_op jit(solution)/shard_map/all_to_all | solution.py:66
  73.8 12.9 %all-to-all-start.2 = ((bf16[4,4,1,22,88]{4,1,3,2,0:T(4,128)(2,1)}), bf16[4,4,1,22,88]{4,1,3,2,0:T(4,128)(2,1)S(1)}, u32[]{:S(2)}, u32[]{:S(2)}) async-start(bf16[4,4,1,22,88]{4,1,3,2,0:T(4,128)(2,1)} %copy.91), calls=%async_computation.2 | async-start | bytes 180224 | tf_op jit(solution)/shard_map/all_to_all | solution.py:74
  86.7 10.3 %all-to-all-start.8 = ((bf16[4,4,1,22,88]{4,1,3,2,0:T(4,128)(2,1)}), bf16[4,4,1,22,88]{4,1,3,2,0:T(4,128)(2,1)S(1)}, u32[]{:S(2)}, u32[]{:S(2)}) async-start(bf16[4,4,1,22,88]{4,1,3,2,0:T(4,128)(2,1)} %copy.99), calls=%async_computation.8 | async-start | bytes 180224 | tf_op jit(solution)/shard_map/all_to_all | solution.py:74
  97.0 10.3 %all-to-all-start.14 = ((bf16[4,4,1,22,88]{4,1,3,2,0:T(4,128)(2,1)}), bf16[4,4,1,22,88]{4,1,3,2,0:T(4,128)(2,1)S(1)}, u32[]{:S(2)}, u32[]{:S(2)}) async-start(bf16[4,4,1,22,88]{4,1,3,2,0:T(4,128)(2,1)} %copy.107), calls=%async_computation.14 | async-start | bytes 180224 | tf_op jit(solution)/shard_map/all_to_all | solution.py:74
  107.3 7.1 %all-to-all-start.3 = ((bf16[2,1,352,88]{2,3,1,0:T(8,128)(2,1)}), bf16[2,1,352,88]{2,3,1,0:T(8,128)(2,1)S(1)}, u32[]{:S(2)}, u32[]{:S(2)}) async-start(bf16[2,1,352,88]{2,3,1,0:T(8,128)(2,1)} %copy.93), calls=%async_computation.3 | async-start | bytes 270336 | tf_op jit(solution)/shard_map/all_to_all | solution.py:26
  130.4 13.4 %all-to-all-start.10 = ((bf16[4,2,352,88]{2,3,1,0:T(8,128)(2,1)}), bf16[4,2,352,88]{2,3,1,0:T(8,128)(2,1)S(1)}, u32[]{:S(2)}, u32[]{:S(2)}) async-start(bf16[4,2,352,88]{2,3,1,0:T(8,128)(2,1)} %stack.43), calls=%async_computation.10 | async-start | bytes 1081344 | tf_op jit(solution)/shard_map/all_to_all | solution.py:26
  143.8 6.8 %all-to-all-start.15 = ((bf16[2,1,352,88]{2,3,1,0:T(8,128)(2,1)}), bf16[2,1,352,88]{2,3,1,0:T(8,128)(2,1)S(1)}, u32[]{:S(2)}, u32[]{:S(2)}) async-start(bf16[2,1,352,88]{2,3,1,0:T(8,128)(2,1)} %copy.109), calls=%async_computation.15 | async-start | bytes 270336 | tf_op jit(solution)/shard_map/all_to_all | solution.py:26
  150.6 18.3 %copy-start = (bf16[2,8,352,88]{2,3,1,0:T(8,128)(2,1)S(1)}, bf16[2,8,352,88]{2,3,1,0:T(8,128)(2,1)}, u32[]{:S(2)}) copy-start(bf16[2,8,352,88]{2,3,1,0:T(8,128)(2,1)} %pad_maximum_fusion.1) | copy-start | bytes 2973700
  174.3 13.6 %all-to-all-start.16 = ((bf16[4,2,352,88]{2,3,1,0:T(8,128)(2,1)}), bf16[4,2,352,88]{2,3,1,0:T(8,128)(2,1)}, u32[]{:S(2)}, u32[]{:S(2)}) async-start(bf16[4,2,352,88]{2,3,1,0:T(8,128)(2,1)} %stack.46), calls=%async_computation.16 | async-start | bytes 1081344 | tf_op jit(solution)/shard_map/all_to_all | solution.py:26
  195.9 1.9 copy-start.2
